TPU v7x, 32 devices: a whole 2x2x4 slice. The times are simulated.
32 devices in a mesh: grp: 8 (over z, core), tp: 4 (over y, x).
Axes of the slice: x: 2, y: 2, z: 4, core: 2. Of those that a mesh axis runs over, the one named last changes fastest.
Arguments:
- hidden: bfloat16 [3072, 5120], P('grp'), may hold values from -6 to 6
- merge_weight: bfloat16 [5120, 8192], P(None, 'tp'), may hold values from -0.078125 to 0.078125
- text_embed: bfloat16 [8192, 8192], P('grp', 'tp'), may hold values from -6 to 6
- gain: float32 [8192], P('tp'), may hold values from 0.1 to 1.9
- head_weight: float32 [8192, 19], P('tp'), may hold values from -2 to 2
- owner: int32 [3072, 1], P('grp'), may hold values from 0 to 7; in each aligned block of 384 rows (0 to 383, 384 to 767, ...) at most 96 rows name the same one
- vis_row: int32 [8, 768], P('grp'), may hold values from 0 to 1023, as said below
- lengths: int32 [8], P('grp'), may hold values from 256 to 1024
- labels: int32 [8, 19], replicated, may hold values from 0 to 1, as said below
- targets: float32 [8, 19], P('grp'), may hold values from -4 to 4
Outputs:
- reward: float32 [8, 19], P('grp')
- visual_grad: bfloat16 [3072, 8192], P('grp', 'tp')
- head_grad: float32 [8192, 19], P('tp')
- gain_grad: float32 [8192], P('tp')
Inputs may be any that keep to these rules, and one draw needn't show every extreme that they name: `owner`: in each vision group's 384 rows no sample is named more than 96 times, a bound that some block reaches. `vis_row`: each row holds 768 different positions. `labels`: an objective may be rated by no sample.
All inputs are finite; a program needn't handle non-finite values.
Results may differ from a plain program's by a relative error of at most 0.0035.
Values may be sent and summed in bfloat16 or wider, within the bound.
A program may use at most 128 MiB of HBM per device.

v0:
```python
import jax
import jax.numpy as jnp
from jax import lax
from jax.sharding import PartitionSpec as P

D = 8192


epsilon = 1e-06


def on_device(
    hidden, merge_weight, text_embed, gain, head_weight, owner, vis_row, lengths, labels, targets
):
    groups = lax.axis_size("grp")
    rows_dev = hidden.shape[0]
    capacity = 2 * rows_dev // groups
    width_dev = merge_weight.shape[1]
    positions = text_embed.shape[0]
    objectives = head_weight.shape[1]
    loss_scale = float(positions * groups // 16)
    visual = jnp.dot(hidden, merge_weight, preferred_element_type=jnp.float32).astype(jnp.bfloat16)
    owners = owner[:, 0]
    onehot = (owners[:, None] == jnp.arange(groups, dtype=jnp.int32)[None, :]).astype(jnp.int32)
    slot_rank = jnp.sum(jnp.cumsum(onehot, axis=0) * onehot, axis=1) - 1
    outbox = (
        jnp.zeros((groups, capacity, width_dev), jnp.bfloat16).at[owners, slot_rank].set(visual)
    )
    live_flags = jnp.zeros((groups, capacity), jnp.bfloat16).at[owners, slot_rank].set(1.0)
    arrived, arrived_flags = (
        lax.all_to_all(outbox, "grp", split_axis=0, concat_axis=0, tiled=True),
        lax.all_to_all(live_flags, "grp", split_axis=0, concat_axis=0, tiled=True),
    )
    arrived = arrived.reshape(groups * capacity, width_dev)
    arrived_flags = arrived_flags.reshape(groups * capacity)
    vis_rows = vis_row[0]
    current = text_embed[vis_rows]
    chosen = jnp.where(arrived_flags[:, None] > 0, arrived, current)
    xfull = text_embed.at[vis_rows].set(chosen).astype(jnp.float32)
    row_sq = jnp.sum(xfull * xfull, axis=1)
    partial_value = jnp.dot(xfull * gain[None, :], head_weight, precision=lax.Precision.HIGHEST)
    length = lengths[0]
    live_rows = (jnp.arange(positions, dtype=jnp.int32) < length).astype(jnp.float32)
    counts = jnp.sum(labels.astype(jnp.float32), axis=0)
    marks = lax.dynamic_index_in_dim(labels, lax.axis_index("grp"), 0, keepdims=False).astype(
        jnp.float32
    )
    target = targets[0]
    total_sq, total_partial = lax.psum((row_sq, partial_value), "tp")
    inv_rms = lax.rsqrt(total_sq / D + epsilon)
    row_weight = live_rows * inv_rms / length.astype(jnp.float32)
    reward = jnp.sum(row_weight[:, None] * total_partial, axis=0)
    cotangent = loss_scale * marks * (reward - target) / jnp.maximum(counts, 1.0)
    row_dot = jnp.dot(total_partial, cotangent, precision=lax.Precision.HIGHEST)
    head_dir = jnp.dot(head_weight, cotangent, precision=lax.Precision.HIGHEST)
    beta_row = row_weight * inv_rms * inv_rms * row_dot / D
    pooled = jnp.sum(row_weight[:, None] * xfull, axis=0)
    head_grad, gain_grad = lax.psum((jnp.outer(gain * pooled, cotangent), pooled * head_dir), "grp")
    coefs = jnp.stack([row_weight[vis_rows], beta_row[vis_rows]], axis=-1).reshape(
        groups, capacity, 2
    )
    spread = jnp.broadcast_to(cotangent[None, :], (groups, objectives))
    coef_back, cot_back = (
        lax.all_to_all(coefs, "grp", split_axis=0, concat_axis=0, tiled=True),
        lax.all_to_all(spread, "grp", split_axis=0, concat_axis=0, tiled=True),
    )
    own_coefs = coef_back[owners, slot_rank]
    own_dirs = jnp.dot(cot_back[owners], head_weight.T, precision=lax.Precision.HIGHEST)
    visual_grad = (
        own_coefs[:, 0:1] * (gain[None, :] * own_dirs)
        - own_coefs[:, 1:2] * visual.astype(jnp.float32)
    ).astype(jnp.bfloat16)
    return (reward[None, :], visual_grad, head_grad, gain_grad)


def solution(mesh):
    placed = (
        P("grp", None),
        P(None, "tp"),
        P("grp", "tp"),
        P("tp"),
        P("tp", None),
        P("grp", None),
        P("grp", None),
        P("grp"),
        P(),
        P("grp", None),
    )
    return jax.shard_map(
        on_device,
        mesh=mesh,
        in_specs=placed,
        out_specs=(P("grp", None), P("grp", "tp"), P("tp", None), P("tp")),
        check_vma=False,
    )
```

profile of v0, /device:TPU:0, one launch (start us, length us, event | category | flops | bytes accessed | tf_op | source)
XLA Modules:
  0.0 366.5 jit_solution(327374665882665979)
XLA Ops:
  7.2 0.0 copy-start
  7.2 0.0 copy-start.6
  7.2 4.7 %copy.29 = bf16[1024,2048]{1,0:T(8,128)(2,1)} copy(bf16[1024,2048]{1,0:T(8,128)(2,1)} %param.12) | data formatting | bytes 8388608
  11.9 0.0 copy-done.6
  12.0 0.9 reduce-window.6
  12.8 0.2 slice_reduce_fusion.2
  13.1 0.1 fusion.4
  13.2 18.5 %scatter_fusion = bf16[8,96]{1,0:T(8,128)(2,1)S(1)} fusion(bf16[8,96]{1,0:T(8,128)(2,1)S(1)} %broadcast_in_dim.18, s32[384]{0:T(512)S(1)} %get-tuple-element.7, bf16[384]{0:T(512)(128)(2,1)S(1)} %broadcast.168), kind=kCustom, calls=%fused_computation.5 | custom fusion | bytes 5376 | tf_op jit(solution)/shard_map/scatter | solution.py:29
  31.8 0.6 copy.19
  32.4 6.4 %all-to-all-start = ((bf16[8,1,96]{2,1,0:T(2,128)(2,1)}), bf16[8,1,96]{2,1,0:T(2,128)(2,1)S(1)}, u32[]{:S(2)}, u32[]{:S(2)}) async-start(bf16[8,1,96]{2,1,0:T(2,128)(2,1)} %copy.19), calls=%async_computation | async-start | bytes 8192 | tf_op jit(solution)/shard_map/all_to_all | solution.py:32
  38.7 13.6 %convolution_convert_fusion = bf16[384,2048]{1,0:T(8,128)(2,1)S(1)} fusion(bf16[384,5120]{1,0:T(8,128)(2,1)} %param.10, bf16[5120,2048]{1,0:T(8,128)(2,1)} %param.11), kind=kOutput, calls=%fused_computation.17 | convolution fusion | flops 8053850112 | bytes 26476544 | tf_op jit(solution)/shard_map/dot_general | solution.py:22
  52.3 0.0 copy-start.1
  52.4 2.2 broadcast_in_dim.21
  54.6 69.1 %scatter_fusion.1 = bf16[8,96,2048]{2,1,0:T(8,128)(2,1)} fusion(bf16[8,96,2048]{2,1,0:T(8,128)(2,1)} %broadcast_in_dim.21, s32[384]{0:T(512)S(1)} %get-tuple-element.7, bf16[384,2048]{1,0:T(8,128)(2,1)S(1)} %convolution_convert_fusion), kind=kCustom, calls=%fused_computation.6 | custom fusion | bytes 4721664 | tf_op jit(solution)/shard_map/scatter | solution.py:27
  123.7 0.0 copy-done.1
  123.7 0.0 all-to-all-done
  123.7 5.0 %all-to-all-start.1 = ((bf16[8,96,2048]{2,1,0:T(8,128)(2,1)}), bf16[8,96,2048]{2,1,0:T(8,128)(2,1)S(1)}, u32[]{:S(2)}, u32[]{:S(2)}) async-start(bf16[8,96,2048]{2,1,0:T(8,128)(2,1)} %scatter_fusion.1), calls=%async_computation.1 | async-start | bytes 6291456 | tf_op jit(solution)/shard_map/all_to_all | solution.py:31
  128.7 0.2 all-reduce.3.cloned.1.call-start
  129.6 0.0 copy-done.8
  129.6 0.0 copy-start.5
  129.6 9.9 %gather_fusion = bf16[768,2048]{1,0:T(8,128)(2,1)} fusion(bf16[1024,2048]{1,0:T(8,128)(2,1)} %copy.29, s32[1024]{0:T(1024)S(1)} %pad_clamp_fusion.1), kind=kCustom, calls=%fused_computation | custom fusion | bytes 6294528 | tf_op jit(solution)/shard_map/gather | solution.py:37
  139.5 0.0 copy-done.5
  139.5 0.1 gt.16
  139.6 60.6 %all-to-all-done.1 = bf16[8,96,2048]{2,1,0:T(8,128)(2,1)S(1)} async-done(((bf16[8,96,2048]{2,1,0:T(8,128)(2,1)}), bf16[8,96,2048]{2,1,0:T(8,128)(2,1)S(1)}, u32[]{:S(2)}, u32[]{:S(2)}) %all-to-all-start.1) | async-done | bytes 3145760 | tf_op jit(solution)/shard_map/all_to_all | solution.py:31
  200.2 4.0 %bitcast_select_fusion = bf16[768,2048]{1,0:T(8,128)(2,1)} fusion(bf16[768,2048]{1,0:T(8,128)(2,1)} %gather_fusion, bf16[8,96,2048]{2,1,0:T(8,128)(2,1)S(1)} %all-to-all-done.1, pred[768]{0:T(1024)(128)(4,1)S(1)} %gt.16), kind=kLoop, calls=%fused_computation.15 | loop fusion | flops 1572864 | bytes 9437952 | tf_op jit(solution)/shard_map/jit(_where)/select_n | solution.py:38
  204.2 12.5 %scatter_fusion.2 = bf16[1024,2048]{1,0:T(8,128)(2,1)} fusion(bf16[1024,2048]{1,0:T(8,128)(2,1)} %copy.29, s32[768]{0:T(1024)S(1)} %fusion.8, bf16[768,2048]{1,0:T(8,128)(2,1)} %bitcast_select_fusion), kind=kCustom, calls=%fused_computation.7 | custom fusion | bytes 9440256 | tf_op jit(solution)/shard_map/scatter | solution.py:39
  216.7 3.1 fusion
  219.8 9.9 %psum.28 = f32[1024]{0:T(1024)S(1)} all-reduce(f32[1024]{0:T(1024)S(1)} %fusion), channel_id=1, replica_groups=mesh['grp'=8,'tp'=4] {'tp'}, use_global_device_ids=true, to_apply=%region_7.8 | all-reduce | flops 1024 | bytes 8192 | tf_op jit(solution)/shard_map/psum | solution.py:49
  229.7 0.0 copy-done
  229.7 0.0 copy-done.3
  229.7 9.9 %fusion.1 = f32[1024,19]{0,1:T(8,128)} fusion(f32[2048,19]{0,1:T(8,128)S(1)} %copy-done, bf16[1024,2048]{1,0:T(8,128)(2,1)} %scatter_fusion.2, f32[2048]{0:T(1024)S(1)} %copy-done.3), kind=kOutput, calls=%fused_computation.12 | convolution fusion | flops 482344960 | bytes 4435968 | tf_op jit(solution)/shard_map/dot_general | solution.py:41
  239.6 0.0 all-reduce.3.cloned.1.call-update
  239.7 3.1 fusion.2
  242.8 0.0 copy-start.7
  242.8 3.2 gather_fusion.1
  246.0 0.1 stack.9
  246.0 32.9 %all-reduce.3.cloned.1.call-done = f32[1024,19]{0,1:T(8,128)} async-done(((f32[1024,19]{0,1:T(8,128)}), f32[1024,19]{0,1:T(8,128)}) %all-reduce.3.cloned.1.call-update) | async-done | bytes 77840 | tf_op jit(solution)/shard_map/psum | solution.py:49
  279.0 1.0 multiply_reduce_fusion
  280.0 0.0 copy-done.7
  280.0 0.0 copy-start.4
  280.0 0.2 fusion.11
  280.2 1.1 fusion.13
  281.4 3.2 gather_fusion.2
  284.5 0.0 copy-start.2
  284.6 0.1 stack.10
  284.6 0.6 broadcast_in_dim.23
  285.2 4.6 %all-to-all-start.3 = ((f32[8,1,19]{2,1,0:T(1,128)}), f32[8,1,19]{2,1,0:T(1,128)S(1)}, u32[]{:S(2)}, u32[]{:S(2)}) async-start(f32[8,1,19]{2,1,0:T(1,128)} %broadcast_in_dim.23), calls=%async_computation.3 | async-start | bytes 8192 | tf_op jit(solution)/shard_map/all_to_all | solution.py:65
  289.9 0.6 copy.20
  290.5 4.9 %all-to-all-done.3 = f32[8,1,19]{2,1,0:T(1,128)S(1)} async-done(((f32[8,1,19]{2,1,0:T(1,128)}), f32[8,1,19]{2,1,0:T(1,128)S(1)}, u32[]{:S(2)}, u32[]{:S(2)}) %all-to-all-start.3) | async-done | bytes 640 | tf_op jit(solution)/shard_map/all_to_all | solution.py:65
  295.3 3.3 all-to-all-start.2
  298.7 0.0 all-reduce.5.cloned.1.call-start
  298.7 0.8 broadcast_multiply_fusion
  299.5 0.0 all-reduce.5.cloned.1.call-update
  299.5 17.9 %psum.31 = f32[2048]{0:T(1024)} all-reduce(f32[2048]{0:T(1024)S(1)} %get-tuple-element.9), channel_id=1, replica_groups=mesh['grp'=8,'tp'=4] {'grp'}, use_global_device_ids=true, to_apply=%region_13.14 | all-reduce | flops 2048 | bytes 16384 | tf_op jit(solution)/shard_map/psum | solution.py:58
  317.4 1.1 gather_fusion.4
  318.5 0.0 copy-done.4
  318.5 0.0 all-to-all-done.2
  318.5 0.2 copy.21
  318.7 3.7 %gather_fusion.3 = f32[384,2]{1,0:T(8,128)S(1)} fusion(f32[8,96,2]{2,1,0:T(8,128)S(1)} %copy.21, s32[384]{0:T(512)S(1)} %get-tuple-element.6), kind=kCustom, calls=%fused_computation.3 | custom fusion | bytes 9216 | tf_op jit(solution)/shard_map/gather | solution.py:67
  322.5 0.3 slice_reduce_fusion.1
  322.7 0.0 copy-done.2
  322.7 4.0 %subtract_convert_fusion = bf16[384,2048]{1,0:T(8,128)(2,1)} fusion(bf16[384,2048]{1,0:T(8,128)(2,1)S(1)} %copy-done.2, f32[384,19]{1,0:T(8,128)S(1)} %gather_fusion.4, f32[2048,19]{0,1:T(8,128)S(1)} %copy-done, f32[384]{0:T(512)S(1)} %get-tuple-element.5, f32[2048]{0:T(1024)S(1)} %copy-done.3, f32[384]{0:T(512)S(1)} %get-tuple-element.4), kind=kOutput, calls=%fused_computation.16 | convolution fusion | flops 184025088 | bytes 3341824 | tf_op jit(solution)/shard_map/dot_general | solution.py:68
  326.7 31.4 %all-reduce.5.cloned.1.call-done = f32[2048,19]{0,1:T(8,128)} async-done(((f32[2048,19]{0,1:T(8,128)}), f32[2048,19]{0,1:T(8,128)}) %all-reduce.5.cloned.1.call-update) | async-done | bytes 155664 | tf_op jit(solution)/shard_map/psum | solution.py:58
  358.0 1.6 copy.30
  (19 shorter events, 0.2 us)
Async XLA Ops:
  7.2 222.5 %copy-start = (f32[2048,19]{0,1:T(8,128)S(1)}, f32[2048,19]{0,1:T(8,128)}, u32[]{:S(2)}) copy-start(f32[2048,19]{0,1:T(8,128)} %param.14) | copy-start | bytes 466948
  7.2 4.8 %copy-start.6 = (s32[384,1]{0,1:T(1,128)S(1)}, s32[384,1]{0,1:T(1,128)}, u32[]{:S(2)}) copy-start(s32[384,1]{0,1:T(1,128)} %param.15) | copy-start | bytes 4612
  32.4 91.3 %all-to-all-start = ((bf16[8,1,96]{2,1,0:T(2,128)(2,1)}), bf16[8,1,96]{2,1,0:T(2,128)(2,1)S(1)}, u32[]{:S(2)}, u32[]{:S(2)}) async-start(bf16[8,1,96]{2,1,0:T(2,128)(2,1)} %copy.19), calls=%async_computation | async-start | bytes 8192 | tf_op jit(solution)/shard_map/all_to_all | solution.py:32
  52.3 71.4 %copy-start.1 = (bf16[384,2048]{1,0:T(8,128)(2,1)}, bf16[384,2048]{1,0:T(8,128)(2,1)S(1)}, u32[]{:S(2)}) copy-start(bf16[384,2048]{1,0:T(8,128)(2,1)S(1)} %convolution_convert_fusion) | copy-start | bytes 4718596
  123.7 5.8 %copy-start.8 = (s32[1,768]{1,0:T(1,128)S(1)}, s32[1,768]{1,0:T(1,128)}, u32[]{:S(2)}) copy-start(s32[1,768]{1,0:T(1,128)} %param.16) | copy-start | bytes 9220
  123.7 76.5 %all-to-all-start.1 = ((bf16[8,96,2048]{2,1,0:T(8,128)(2,1)}), bf16[8,96,2048]{2,1,0:T(8,128)(2,1)S(1)}, u32[]{:S(2)}, u32[]{:S(2)}) async-start(bf16[8,96,2048]{2,1,0:T(8,128)(2,1)} %scatter_fusion.1), calls=%async_computation.1 | async-start | bytes 6291456 | tf_op jit(solution)/shard_map/all_to_all | solution.py:31
  128.7 150.3 %all-reduce.3.cloned.1.call-start = ((), (), s32[]{:S(2)}) async-start(), calls=%async_computation.4 | async-start | bytes 196608 | tf_op jit(solution)/shard_map/psum | solution.py:49
  129.6 9.9 %copy-start.5 = (s32[8,19]{1,0:T(8,128)S(1)}, s32[8,19]{1,0:T(8,128)}, u32[]{:S(2)}) copy-start(s32[8,19]{1,0:T(8,128)} %param.18) | copy-start | bytes 1828
  216.7 13.0 %copy-start.3 = (f32[2048]{0:T(1024)S(1)}, f32[2048]{0:T(1024)}, u32[]{:S(2)}) copy-start(f32[2048]{0:T(1024)} %param.13) | copy-start | bytes 24580
  242.8 37.2 %copy-start.7 = (f32[1,19]{1,0:T(1,128)S(1)}, f32[1,19]{1,0:T(1,128)}, u32[]{:S(2)}) copy-start(f32[1,19]{1,0:T(1,128)} %param.19) | copy-start | bytes 232
  280.0 38.5 %copy-start.4 = (f32[19]{0:T(128)}, f32[19]{0:T(128)S(1)}, u32[]{:S(2)}) copy-start(f32[19]{0:T(128)S(1)} %multiply_reduce_fusion) | copy-start | bytes 232
  284.5 38.2 %copy-start.2 = (bf16[384,2048]{1,0:T(8,128)(2,1)S(1)}, bf16[384,2048]{1,0:T(8,128)(2,1)}, u32[]{:S(2)}) copy-start(bf16[384,2048]{1,0:T(8,128)(2,1)} %copy-done.1) | copy-start | bytes 4718596
  285.2 10.1 %all-to-all-start.3 = ((f32[8,1,19]{2,1,0:T(1,128)}), f32[8,1,19]{2,1,0:T(1,128)S(1)}, u32[]{:S(2)}, u32[]{:S(2)}) async-start(f32[8,1,19]{2,1,0:T(1,128)} %broadcast_in_dim.23), calls=%async_computation.3 | async-start | bytes 8192 | tf_op jit(solution)/shard_map/all_to_all | solution.py:65
  295.3 23.2 %all-to-all-start.2 = ((f32[8,96,2]{1,2,0:T(2,128)}), f32[8,96,2]{1,2,0:T(2,128)S(1)}, u32[]{:S(2)}, u32[]{:S(2)}) async-start(f32[8,96,2]{1,2,0:T(2,128)} %copy.20), calls=%async_computation.2 | async-start | bytes 16384 | tf_op jit(solution)/shard_map/all_to_all | solution.py:64
  298.7 59.4 %all-reduce.5.cloned.1.call-start = ((), (), s32[]{:S(2)}) async-start(), calls=%async_computation.5 | async-start | bytes 393216 | tf_op jit(solution)/shard_map/psum | solution.py:58
Sparse Core Ops, SparseCore 0:
  239.8 39.1 all-reduce.2
  302.4 55.6 all-reduce.4
where the time goes:
time: 369 us; the launch traced here: 366 us
  local copies, waits for them, and re-layouts  133 us (36%)
  waiting for transfers between devices  130 us (35%)
  matrix products  28.8 us (8%)
  blocking collectives  27.8 us (8%)
  starting transfers between devices  19.5 us (5%)
  between operations  14.9 us (4%)
  other arithmetic  13.1 us (4%)
    scatter x1, local copies, waits for them, and re-layouts, on_device(): jnp.zeros((groups, capacity, width_dev), jnp.bfloat16).at[owners, slot_rank]  69.1 us
    all_to_all x1, waiting for transfers between devices, on_device(): lax.all_to_all(outbox, 'grp', split_axis=0, concat_axis=0, tiled=True)  60.6 us
    psum x1, waiting for transfers between devices, on_device(): total_sq, total_partial = lax.psum((row_sq, partial_value), 'tp')  32.9 us
    psum x1, waiting for transfers between devices, on_device(): lax.psum((jnp.outer(gain * pooled, cotangent), pooled * head_dir), 'grp')  31.4 us
    scatter x1, local copies, waits for them, and re-layouts, on_device(): jnp.zeros((groups, capacity), jnp.bfloat16).at[owners, slot_rank].set(1.0)  18.5 us
    psum x1, blocking collectives, on_device(): lax.psum((jnp.outer(gain * pooled, cotangent), pooled * head_dir), 'grp')  17.9 us
    dot_general x1, matrix products, on_device(): jnp.dot(hidden, merge_weight, preferred_element_type=jnp.float32)  13.6 us
    scatter x1, local copies, waits for them, and re-layouts, on_device(): xfull = text_embed.at[vis_rows].set(chosen).astype(jnp.float32)  12.5 us
  transfers between devices with their start and end apart: 6, of which 4 were waited for; matrix products, arithmetic and copies ran while one was open for 31% of the time, Pallas kernels for 0%

commit v1 on v0

v1 whole, which is shorter than its diff:
```python
import functools

import jax
import jax.numpy as jnp
from jax import lax
from jax.experimental import pallas as pl
from jax.experimental.pallas import tpu as pltpu
from jax.sharding import PartitionSpec as P

EPS = 1e-06
CW = 256
F32 = jnp.float32
BF16 = jnp.bfloat16
MESH = pl.DeviceIdType.MESH
HI = lax.Precision.HIGHEST


def iota(shape, dim):
    return lax.broadcasted_iota(jnp.int32, shape, dim)


def dot(a, b, ca, cb, precision=None):
    return lax.dot_general(
        a, b, (((ca,), (cb,)), ((), ())), precision=precision, preferred_element_type=F32
    )


def split2(a):
    hi = a.astype(BF16).astype(F32)
    return hi, a - hi


def split3(a):
    hi, rest = split2(a)
    mid, low = split2(rest)
    return hi, mid, low


def kernel(
    G, T, cap, scale, K, KR,
    hid_hbm, w_hbm, txt_hbm, gain_ref, hwt_ref, own_ref, vis_ref, len_ref, lab_ref, tgt_ref,
    rew_ref, vg_hbm, head_ref, gg_ref,
    hid, wv, tx, xs, og, ghp, gh3, pacc, sqacc, tsq, pk, tsqx, vst, rbuf, zsend, zrecv, zall, ztx,
    in_sem, w_sem, t_sem, o_sem,
    pk_s, pk_r, ts_s, ts_r, vs_s, vs_r, rb_s, rb_r, zs_s, zs_r, za_s, za_r,
):
    M, H = hid.shape
    Fd = tx.shape[1]
    Pn = tx.shape[0]
    SL = vis_ref.shape[1]
    KB = gh3.shape[0] // 3
    N = Fd // CW
    D = Fd * T
    nA = N // 2
    nM = (N - nA) // 2
    nB = N - nA - nM
    RB = Pn // nA
    CB = Fd // nB // 128 * 128
    me = lax.axis_index("grp")
    mt = lax.axis_index("tp")

    pltpu.make_async_copy(hid_hbm, hid, in_sem).start()

    def wcopy(n):
        return pltpu.make_async_copy(
            w_hbm.at[:, pl.ds(pl.multiple_of(n * CW, CW), CW)],
            wv.at[n], w_sem.at[n])

    def tcopy(n):
        rows = pl.ds(pl.multiple_of(n * RB, RB), RB)
        return pltpu.make_async_copy(txt_hbm.at[rows, :], tx.at[rows, :], t_sem.at[n])

    for n in range(N):
        wcopy(n).start()
        if n < nA:
            tcopy(n).start()

    bar = pltpu.get_barrier_semaphore()

    def greet_g(i, c):
        pl.semaphore_signal(bar, inc=1, device_id=(lax.rem(me + i, G), mt), device_id_type=MESH)
        return c

    def greet_t(i, c):
        pl.semaphore_signal(bar, inc=1, device_id=(me, lax.rem(mt + i, T)), device_id_type=MESH)
        return c

    lax.fori_loop(1, G, greet_g, 0)
    lax.fori_loop(1, T, greet_t, 0)

    def grp_copy(src, dst, ss, rs, i):
        peer = lax.rem(me + i, G)
        return pltpu.make_async_remote_copy(
            src, dst, ss.at[i], rs, device_id=(peer, mt), device_id_type=MESH)

    def g_gather(buf, ss, rs, i):
        return grp_copy(buf.at[me], buf.at[me], ss, rs.at[me], i)

    def g_gather_in(buf, ss, rs, i):
        peer = lax.rem(me + i, G)
        return grp_copy(buf.at[peer], buf.at[peer], ss, rs.at[peer], i)

    def t_gather(buf, ss, rs, i, slot):
        return pltpu.make_async_remote_copy(
            buf.at[slot], buf.at[slot], ss.at[i], rs.at[slot],
            device_id=(me, lax.rem(mt + i, T)), device_id_type=MESH)

    def loop(n, f):
        def body(i, c):
            f(i)
            return c
        lax.fori_loop(1, n, body, 0)

    own = own_ref[...]
    oht = (jnp.broadcast_to(own, (G, M)) == iota((G, M), 0)).astype(F32)
    before = (iota((M, M), 0) < iota((M, M), 1)).astype(F32).astype(BF16)
    ohb = oht.astype(BF16)
    rank = jnp.sum(oht * dot(ohb, before, 1, 0), axis=0, keepdims=True)
    counts = dot(jnp.ones((8, M), F32).astype(BF16), ohb, 1, 1)

    length = len_ref[0]
    inv_len = jnp.full((1, 1), 1.0, F32) / jnp.full((1, 1), length, jnp.int32).astype(F32)
    vis = vis_ref[...]
    live = jnp.where(vis < length, jnp.broadcast_to(inv_len, vis.shape), 0.0)
    pk[me] = jnp.zeros(pk.shape[1:], F32)
    pk[me, 0:1, :] = live
    pk[me, 1:2, 0:G] = counts[0:1, :]
    pk[me, 2:3, 0:K] = tgt_ref[...]
    pl.semaphore_wait(bar, G - 1 + T - 1)
    loop(G, lambda i: g_gather(pk, pk_s, pk_r, i).start())

    ghp[...] = jnp.zeros(ghp.shape, F32)
    ghp[0:K, :] = hwt_ref[...] * gain_ref[...]
    hi, mid, low = split3(ghp[...])
    gh3[0:KB, :] = hi.astype(BF16)
    gh3[KB:2 * KB, :] = mid.astype(BF16)
    gh3[2 * KB:3 * KB, :] = low.astype(BF16)
    pacc[...] = jnp.zeros(pacc.shape, F32)
    sqacc[...] = jnp.zeros(sqacc.shape, F32)
    pltpu.make_async_copy(hid_hbm, hid, in_sem).wait()

    def project(n):
        wcopy(n).wait()
        cols = pl.ds(pl.multiple_of(n * CW, CW), CW)
        x = jnp.dot(hid[...], wv[n], preferred_element_type=F32).astype(BF16)
        xs[:, cols] = x
        pacc[...] += dot(gh3[:, cols], x, 1, 1)
        xf = x.astype(F32)
        sq = xf * xf
        sqacc[...] += functools.reduce(
            lambda a, b: a + b, [sq[:, c:c + 128] for c in range(0, CW, 128)])

    def phase_a(n, c):
        project(n)
        tcopy(n).wait()
        rows = pl.ds(pl.multiple_of(n * RB, RB), RB)
        acc = None
        for t in range(0, Fd, 128):
            xf = tx[rows, t:t + 128].astype(F32)
            acc = xf * xf if acc is None else acc + xf * xf
        tsq[rows, :] = acc
        return c

    lax.fori_loop(0, nA, phase_a, 0)
    tsum = jnp.sum(tsq[...].T, axis=0, keepdims=True)
    tsqx[mt] = jnp.broadcast_to(tsum, (8, Pn))
    loop(T, lambda i: t_gather(tsqx, ts_s, ts_r, i, mt).start())

    def phase_m(n, c):
        project(n)
        return c

    lax.fori_loop(nA, nA + nM, phase_m, 0)

    loop(G, lambda i: g_gather_in(pk, pk_s, pk_r, i).wait_recv())
    loop(T, lambda i: t_gather(tsqx, ts_s, ts_r, i, lax.rem(mt + i, T)).wait_recv())
    cnt_of = jnp.sum(
        jnp.where(iota((G, 128), 1) == me, pk[:, 1, 0:128], 0.0), axis=1, keepdims=True)
    slot = iota((G, SL), 1) - iota((G, SL), 0) * cap
    held = jnp.max(
        jnp.where((slot >= 0) & (slot < cnt_of.astype(jnp.int32)), 1.0, 0.0),
        axis=0, keepdims=True)
    visf = jnp.where(held > 0, vis.astype(F32), -1.0)
    vist = jnp.broadcast_to(visf, (128, SL)).T
    dead = []
    for b in range(0, Pn, 128):
        pos = (iota((SL, 128), 1) + b).astype(F32)
        dead.append(jnp.max(jnp.where(vist == pos, 1.0, 0.0), axis=0, keepdims=True))
    dead = jnp.concatenate(dead, axis=1)
    tot = tsqx[0][0:1, :]
    for i in range(1, T):
        tot = tot + tsqx[i][0:1, :]
    tw = jnp.where(
        (iota((1, Pn), 1) < length) & (dead == 0), lax.rsqrt(tot / D + EPS) * inv_len, 0.0)
    th, tm, tl = split3(jnp.broadcast_to(tw, (8, Pn)))
    row8 = iota((8, Pn), 0)
    tw3 = jnp.where(
        row8 == 0, th, jnp.where(row8 == 1, tm, jnp.where(row8 == 2, tl, 0.0))).astype(BF16)

    def phase_b(n, c):
        project(n)
        cols = pl.ds(pl.multiple_of((n - nA - nM) * CB, 128), CB)
        z3 = jnp.dot(tw3, tx[:, cols], preferred_element_type=F32)
        ztx[:, cols] = jnp.broadcast_to(jnp.sum(z3, axis=0, keepdims=True), (8, CB))
        return c

    lax.fori_loop(nA + nM, N, phase_b, 0)
    trew = dot(ztx[...], ghp[...], 1, 1, HI)

    sq = jnp.sum(sqacc[...].T, axis=0, keepdims=True)
    pt = pacc[0:KB, :] + pacc[KB:2 * KB, :] + pacc[2 * KB:3 * KB, :]
    vst[mt] = jnp.zeros(vst.shape[1:], F32)
    vst[mt, 0:KR, :] = pt[0:KR, :]
    vst[mt, K:K + 1, :] = sq
    vst[mt, KR:KR + 8, 0:KB] = trew
    loop(T, lambda i: t_gather(vst, vs_s, vs_r, i, mt).start())

    lg = pk[:, 0, :]
    sel = dot(lg, oht, 0, 0, HI)
    at = rank.astype(jnp.int32) + me * cap
    ltok = jnp.sum(jnp.where(iota((SL, M), 0) == at, sel, 0.0), axis=0, keepdims=True)
    loop(T, lambda i: t_gather(vst, vs_s, vs_r, i, lax.rem(mt + i, T)).wait_recv())
    st = vst[0]
    for i in range(1, T):
        st = st + vst[i]
    ptot = st[0:KR, :]
    inv = lax.rsqrt(st[K:K + 1, :] / D + EPS)
    w = inv * ltok
    wt = oht * w
    rpart = dot(wt, ptot, 1, 1, HI)
    mine = iota((G, KR), 0) == me
    rbuf[me] = jnp.zeros(rbuf.shape[1:], F32)
    rbuf[me, :, 0:KR] = rpart + jnp.where(mine, st[KR:KR + 1, 0:KR], 0.0)
    loop(G, lambda i: g_gather(rbuf, rb_s, rb_r, i).start())

    wh, wm, wl = split3(wt)
    w3 = jnp.concatenate([wh, wm, wl], axis=0).astype(BF16)
    z3 = jnp.dot(w3, xs[...], preferred_element_type=F32)
    z = z3[0:G] + z3[G:2 * G] + z3[2 * G:3 * G]
    z = z + jnp.where(iota((G, Fd), 0) == me, ztx[0:1, :], 0.0)
    for t in range(Fd // 128):
        zsend[:, t, :] = z[:, t * 128:(t + 1) * 128]

    def zscatter(i):
        peer = lax.rem(me + i, G)
        return grp_copy(zsend.at[peer], zrecv.at[me], zs_s, zs_r.at[me], i)

    def zscatter_in(i):
        peer = lax.rem(me + i, G)
        return grp_copy(zsend.at[peer], zrecv.at[peer], zs_s, zs_r.at[peer], i)

    loop(G, lambda i: zscatter(i).start())
    zrecv[me] = zsend[me]

    loop(G, lambda i: g_gather_in(rbuf, rb_s, rb_r, i).wait_recv())
    rew = rbuf[0]
    for i in range(1, G):
        rew = rew + rbuf[i]
    rew = rew[:, 0:K]
    rew_ref[...] = jnp.sum(
        jnp.where(iota((G, K), 0) == me, rew, 0.0), axis=0, keepdims=True)
    marks = lab_ref[...].astype(F32)
    total = jnp.maximum(jnp.sum(marks, axis=0, keepdims=True), 1.0)
    cot = scale * marks * (rew - pk[:, 2, 0:K]) / total
    v = dot(cot, hwt_ref[...], 1, 0, HI)
    arow = jnp.sum(ptot[0:K, :] * dot(cot, oht, 0, 0, HI), axis=0, keepdims=True)
    beta = w * inv * inv * arow / D
    bcol = jnp.broadcast_to(beta, (128, M)).T

    loop(G, lambda i: zscatter_in(i).wait_recv())
    zs = zrecv[0]
    for i in range(1, G):
        zs = zs + zrecv[i]
    zall[me] = zs
    loop(G, lambda i: g_gather(zall, za_s, za_r, i).start())

    gv = gain_ref[...] * v
    gh, gl = split2(gv)
    lhs = jnp.concatenate([wh, wm, wh], axis=0).astype(BF16)
    og_rhs = jnp.concatenate([gh, gh, gl], axis=0).astype(BF16)
    bfull = jnp.concatenate([bcol] * (CW // 128), axis=1)

    def ocopy(n):
        cols = slice(n * CW, (n + 1) * CW)
        return pltpu.make_async_copy(og.at[:, cols], vg_hbm.at[:, cols], o_sem.at[n])

    for n in range(N):
        cols = slice(n * CW, (n + 1) * CW)
        part = dot(lhs, og_rhs[:, cols], 0, 0)
        og[:, cols] = (part - bfull * xs[:, cols].astype(F32)).astype(BF16)
        ocopy(n).start()

    loop(G, lambda i: g_gather_in(zall, za_s, za_r, i).wait_recv())
    zf = jnp.concatenate([zall[:, t, :] for t in range(Fd // 128)], axis=1)
    head_ref[...] = gain_ref[...] * dot(cot, zf, 0, 0, HI)
    gg_ref[...] = jnp.sum(zf * v, axis=0, keepdims=True)

    for n in range(N):
        ocopy(n).wait()
    loop(G, lambda i: g_gather(pk, pk_s, pk_r, i).wait_send())
    loop(T, lambda i: t_gather(tsqx, ts_s, ts_r, i, mt).wait_send())
    loop(T, lambda i: t_gather(vst, vs_s, vs_r, i, mt).wait_send())
    loop(G, lambda i: g_gather(rbuf, rb_s, rb_r, i).wait_send())
    loop(G, lambda i: zscatter(i).wait_send())
    loop(G, lambda i: g_gather(zall, za_s, za_r, i).wait_send())


def on_device(
    hidden, merge_weight, text_embed, gain, head_weight, owner, vis_row, lengths, labels, targets
):
    G = lax.axis_size("grp")
    T = lax.axis_size("tp")
    M, H = hidden.shape
    cap = 2 * M // G
    Pn, Fd = text_embed.shape
    K = head_weight.shape[1]
    SL = vis_row.shape[1]
    KR = (K + 1 + 7) // 8 * 8
    KB = (KR + 15) // 16 * 16
    N = Fd // CW
    nA = N // 2
    scale = float(Pn * G // 16)
    vmem = pl.BlockSpec(memory_space=pltpu.VMEM)
    hbm = pl.BlockSpec(memory_space=pl.ANY)
    dma = pltpu.SemaphoreType.DMA
    reward, grad, head, gg = pl.pallas_call(
        functools.partial(kernel, G, T, cap, scale, K, KR),
        name="relay",
        out_shape=(
            jax.ShapeDtypeStruct((1, K), F32),
            jax.ShapeDtypeStruct((M, Fd), BF16),
            jax.ShapeDtypeStruct((K, Fd), F32),
            jax.ShapeDtypeStruct((1, Fd), F32),
        ),
        in_specs=[hbm, hbm, hbm, vmem, vmem, vmem, vmem,
                  pl.BlockSpec(memory_space=pltpu.SMEM), vmem, vmem],
        out_specs=(vmem, hbm, vmem, vmem),
        scratch_shapes=[
            pltpu.VMEM((M, H), BF16),
            pltpu.VMEM((N, H, CW), BF16),
            pltpu.VMEM((Pn, Fd), BF16),
            pltpu.VMEM((M, Fd), BF16),
            pltpu.VMEM((M, Fd), BF16),
            pltpu.VMEM((KB, Fd), F32),
            pltpu.VMEM((3 * KB, Fd), BF16),
            pltpu.VMEM((3 * KB, M), F32),
            pltpu.VMEM((M, 128), F32),
            pltpu.VMEM((Pn, 128), F32),
            pltpu.VMEM((G, 8, SL), F32),
            pltpu.VMEM((T, 8, Pn), F32),
            pltpu.VMEM((T, KR + 8, M), F32),
            pltpu.VMEM((G, G, 128), F32),
            pltpu.VMEM((G, Fd // 128, 128), F32),
            pltpu.VMEM((G, Fd // 128, 128), F32),
            pltpu.VMEM((G, Fd // 128, 128), F32),
            pltpu.VMEM((8, Fd), F32),
            dma, dma((N,)), dma((nA,)), dma((N,)),
            dma((G,)), dma((G,)), dma((T,)), dma((T,)), dma((T,)), dma((T,)),
            dma((G,)), dma((G,)), dma((G,)), dma((G,)), dma((G,)), dma((G,)),
        ],
        compiler_params=pltpu.CompilerParams(
            collective_id=0, has_side_effects=True, vmem_limit_bytes=60 * 1024 * 1024),
    )(hidden, merge_weight, text_embed, gain[None, :], head_weight.T, owner.T,
      vis_row, lengths, labels, targets)
    return reward, grad, head.T, gg[0]


def solution(mesh):
    placed = (
        P("grp", None),
        P(None, "tp"),
        P("grp", "tp"),
        P("tp"),
        P("tp", None),
        P("grp", None),
        P("grp", None),
        P("grp"),
        P(),
        P("grp", None),
    )
    return jax.shard_map(
        on_device,
        mesh=mesh,
        in_specs=placed,
        out_specs=(P("grp", None), P("grp", "tp"), P("tp", None), P("tp")),
        check_vma=False,
    )
```

time: 369 us -> 50.1 us (0.14)
  waiting for transfers between devices: 130 us -> 0 us
  local copies, waits for them, and re-layouts: 133 us -> 6.83 us
  Pallas kernels: 0 us -> 41.8 us
  matrix products: 28.8 us -> 0 us
  blocking collectives: 27.8 us -> 0 us
  starting transfers between devices: 19.5 us -> 0 us
  between operations: 14.9 us -> 1.29 us
  other arithmetic: 13.1 us -> 0 us
    scatter x3 -> x0, local copies, waits for them, and re-layouts: 100 us -> none  [the longest x1 69.1 us: on_device(): jnp.zeros((groups, capacity, width_dev), jnp.bfloat16).at[owners, slot_rank]]
    all_to_all x4 -> x0, waiting for transfers between devices: 65.5 us -> none  [the longest x1 60.6 us: on_device(): lax.all_to_all(outbox, 'grp', split_axis=0, concat_axis=0, tiled=True)]
    psum x2 -> x0, waiting for transfers between devices: 64.3 us -> none  [the longest x1 32.9 us: on_device(): total_sq, total_partial = lax.psum((row_sq, partial_value), 'tp')]
    pallas_call x0 -> x1, Pallas kernels: none -> 41.8 us  [on_device(): pl.pallas_call(functools.partial(kernel, G, T, cap, scale, K, KR), name='...]
    dot_general x5 -> x0, matrix products: 28.8 us -> none  [the longest x1 13.6 us: on_device(): jnp.dot(hidden, merge_weight, preferred_element_type=jnp.float32)]
    psum x2 -> x0, blocking collectives: 27.8 us -> none  [the longest x1 17.9 us: on_device(): lax.psum((jnp.outer(gain * pooled, cotangent), pooled * head_dir), 'grp')]
    gather x5 -> x0, local copies, waits for them, and re-layouts: 21.1 us -> none  [the longest x1 9.86 us: on_device(): current = text_embed[vis_rows]]
    all_to_all x4 -> x0, starting transfers between devices: 19.2 us -> none  [the longest x1 6.35 us: on_device(): lax.all_to_all(live_flags, 'grp', split_axis=0, concat_axis=0, tiled=True)]
  transfers between devices with their start and end apart: 6 -> 0, of which waited for: 4 -> 0; matrix products, arithmetic and copies ran while one was open for 31% -> 0% of each run, Pallas kernels for 0% -> 0%
where the time goes in v1:
time: 50.1 us; the launch traced here: 49.9 us
  Pallas kernels  41.8 us (83%)
  local copies, waits for them, and re-layouts  6.83 us (14%)
  between operations  1.29 us (3%)
    pallas_call x1, Pallas kernels, on_device(): pl.pallas_call(functools.partial(kernel, G, T, cap, scale, K, KR), name='...  41.8 us
    unnamed x4, local copies, waits for them, and re-layouts  6.83 us

profile of v1, /device:TPU:0, one launch (start us, length us, event | category | flops | bytes accessed | tf_op | source)
XLA Modules:
  0.0 49.9 jit_solution(15684869332129610945)
XLA Ops:
  1.3 41.8 %relay.1 = (f32[1,19]{1,0:T(1,128)}, bf16[384,2048]{1,0:T(8,128)(2,1)}, f32[19,2048]{1,0:T(8,128)}, f32[1,2048]{1,0:T(1,128)}) custom-call(bf16[384,5120]{1,0:T(8,128)(2,1)} %hid_hbm.1, bf16[5120,2048]{1,0:T(8,128)(2,1)} %w_hbm.1, bf16[1024,2048]{1,0:T(8,128)(2,1)} %txt_hbm.1, f32[1,2048]{1,0:T(1,128)} %bitcast.7, f32[19,2048]{1,0:T(8,128)} %bitcast.5, ...), custom_call_target="tpu_custom_call" | custom-call | tf_op jit(solution)/shard_map/relay/pallas_call | solution.py:326
  43.1 1.2 %copy.19 = f32[1,19]{1,0:T(1,128)} copy(f32[1,19]{1,0:T(1,128)} %get-tuple-element.16) | data formatting | bytes 152
  44.3 2.7 %copy.20 = bf16[384,2048]{1,0:T(8,128)(2,1)} copy(bf16[384,2048]{1,0:T(8,128)(2,1)} %get-tuple-element.17) | data formatting | bytes 3145728
  47.0 1.6 %copy.21 = f32[2048,19]{0,1:T(8,128)} copy(f32[2048,19]{0,1:T(8,128)} %bitcast.6) | data formatting | bytes 311296
  48.6 1.3 %copy.22 = f32[2048]{0:T(1024)} copy(f32[2048]{0:T(1024)} %bitcast.8) | data formatting | bytes 16384

commit v2 on v1

--- a/solution.py
+++ b/solution.py
@@ -39,8 +39,8 @@
 def kernel(
     G, T, cap, scale, K, KR,
     hid_hbm, w_hbm, txt_hbm, gain_ref, hwt_ref, own_ref, vis_ref, len_ref, lab_ref, tgt_ref,
-    rew_ref, vg_hbm, head_ref, gg_ref,
-    hid, wv, tx, xs, og, ghp, gh3, pacc, sqacc, tsq, pk, tsqx, vst, rbuf, zsend, zrecv, zall, ztx,
+    rew_ref, x_hbm, head_ref, gg_ref, lhs_ref, rhs_ref, bcol_ref,
+    hid, wv, tx, xs, ghp, gh3, pacc, sqacc, tsq, pk, tsqx, vst, rbuf, zsend, zrecv, zall, ztx,
     in_sem, w_sem, t_sem, o_sem,
     pk_s, pk_r, ts_s, ts_r, vs_s, vs_r, rb_s, rb_r, zs_s, zs_r, za_s, za_r,
 ):
@@ -139,11 +139,16 @@
     sqacc[...] = jnp.zeros(sqacc.shape, F32)
     pltpu.make_async_copy(hid_hbm, hid, in_sem).wait()
 
+    def xcopy(n):
+        cols = pl.ds(pl.multiple_of(n * CW, CW), CW)
+        return pltpu.make_async_copy(xs.at[:, cols], x_hbm.at[:, cols], o_sem.at[n])
+
     def project(n):
         wcopy(n).wait()
         cols = pl.ds(pl.multiple_of(n * CW, CW), CW)
         x = jnp.dot(hid[...], wv[n], preferred_element_type=F32).astype(BF16)
         xs[:, cols] = x
+        xcopy(n).start()
         pacc[...] += dot(gh3[:, cols], x, 1, 1)
         xf = x.astype(F32)
         sq = xf * xf
@@ -276,19 +281,9 @@
 
     gv = gain_ref[...] * v
     gh, gl = split2(gv)
-    lhs = jnp.concatenate([wh, wm, wh], axis=0).astype(BF16)
-    og_rhs = jnp.concatenate([gh, gh, gl], axis=0).astype(BF16)
-    bfull = jnp.concatenate([bcol] * (CW // 128), axis=1)
-
-    def ocopy(n):
-        cols = slice(n * CW, (n + 1) * CW)
-        return pltpu.make_async_copy(og.at[:, cols], vg_hbm.at[:, cols], o_sem.at[n])
-
-    for n in range(N):
-        cols = slice(n * CW, (n + 1) * CW)
-        part = dot(lhs, og_rhs[:, cols], 0, 0)
-        og[:, cols] = (part - bfull * xs[:, cols].astype(F32)).astype(BF16)
-        ocopy(n).start()
+    lhs_ref[...] = jnp.concatenate([wh, wm, wh], axis=0).astype(BF16)
+    rhs_ref[...] = jnp.concatenate([gh, gh, gl], axis=0).astype(BF16)
+    bcol_ref[...] = bcol
 
     loop(G, lambda i: g_gather_in(zall, za_s, za_r, i).wait_recv())
     zf = jnp.concatenate([zall[:, t, :] for t in range(Fd // 128)], axis=1)
@@ -296,13 +291,39 @@
     gg_ref[...] = jnp.sum(zf * v, axis=0, keepdims=True)
 
     for n in range(N):
-        ocopy(n).wait()
+        xcopy(n).wait()
     loop(G, lambda i: g_gather(pk, pk_s, pk_r, i).wait_send())
     loop(T, lambda i: t_gather(tsqx, ts_s, ts_r, i, mt).wait_send())
     loop(T, lambda i: t_gather(vst, vs_s, vs_r, i, mt).wait_send())
     loop(G, lambda i: g_gather(rbuf, rb_s, rb_r, i).wait_send())
     loop(G, lambda i: zscatter(i).wait_send())
     loop(G, lambda i: g_gather(zall, za_s, za_r, i).wait_send())
+
+
+def finish(
+    x_hbm, lhs_ref, rhs_ref, bcol_ref, rew_in, head_in, gg_in, rew_ref, vg_hbm, head_ref, gg_ref,
+    xv, og, i_sem, o_sem,
+):
+    N = xv.shape[1] // CW
+
+    def move(src, dst, sem, n):
+        cols = slice(n * CW, (n + 1) * CW)
+        return pltpu.make_async_copy(src.at[:, cols], dst.at[:, cols], sem.at[n])
+
+    for n in range(N):
+        move(x_hbm, xv, i_sem, n).start()
+    rew_ref[...] = rew_in[...]
+    head_ref[...] = head_in[...]
+    gg_ref[...] = gg_in[...]
+    bfull = jnp.concatenate([bcol_ref[...]] * (CW // 128), axis=1)
+    for n in range(N):
+        cols = slice(n * CW, (n + 1) * CW)
+        part = dot(lhs_ref[...], rhs_ref[:, cols], 0, 0)
+        move(x_hbm, xv, i_sem, n).wait()
+        og[:, cols] = (part - bfull * xv[:, cols].astype(F32)).astype(BF16)
+        move(og, vg_hbm, o_sem, n).start()
+    for n in range(N):
+        move(og, vg_hbm, o_sem, n).wait()
 
 
 def on_device(
@@ -323,7 +344,7 @@
     vmem = pl.BlockSpec(memory_space=pltpu.VMEM)
     hbm = pl.BlockSpec(memory_space=pl.ANY)
     dma = pltpu.SemaphoreType.DMA
-    reward, grad, head, gg = pl.pallas_call(
+    reward, x, head, gg, lhs, rhs, bcol = pl.pallas_call(
         functools.partial(kernel, G, T, cap, scale, K, KR),
         name="relay",
         out_shape=(
@@ -331,15 +352,17 @@
             jax.ShapeDtypeStruct((M, Fd), BF16),
             jax.ShapeDtypeStruct((K, Fd), F32),
             jax.ShapeDtypeStruct((1, Fd), F32),
+            jax.ShapeDtypeStruct((3 * G, M), BF16),
+            jax.ShapeDtypeStruct((3 * G, Fd), BF16),
+            jax.ShapeDtypeStruct((M, 128), F32),
         ),
         in_specs=[hbm, hbm, hbm, vmem, vmem, vmem, vmem,
                   pl.BlockSpec(memory_space=pltpu.SMEM), vmem, vmem],
-        out_specs=(vmem, hbm, vmem, vmem),
+        out_specs=(vmem, hbm, vmem, vmem, vmem, vmem, vmem),
         scratch_shapes=[
             pltpu.VMEM((M, H), BF16),
             pltpu.VMEM((N, H, CW), BF16),
             pltpu.VMEM((Pn, Fd), BF16),
-            pltpu.VMEM((M, Fd), BF16),
             pltpu.VMEM((M, Fd), BF16),
             pltpu.VMEM((KB, Fd), F32),
             pltpu.VMEM((3 * KB, Fd), BF16),
@@ -362,6 +385,20 @@
             collective_id=0, has_side_effects=True, vmem_limit_bytes=60 * 1024 * 1024),
     )(hidden, merge_weight, text_embed, gain[None, :], head_weight.T, owner.T,
       vis_row, lengths, labels, targets)
+    reward, grad, head, gg = pl.pallas_call(
+        finish,
+        name="finish",
+        out_shape=(
+            jax.ShapeDtypeStruct((1, K), F32),
+            jax.ShapeDtypeStruct((M, Fd), BF16),
+            jax.ShapeDtypeStruct((K, Fd), F32),
+            jax.ShapeDtypeStruct((1, Fd), F32),
+        ),
+        in_specs=[hbm, vmem, vmem, vmem, vmem, vmem, vmem],
+        out_specs=(vmem, hbm, vmem, vmem),
+        scratch_shapes=[
+            pltpu.VMEM((M, Fd), BF16), pltpu.VMEM((M, Fd), BF16), dma((N,)), dma((N,))],
+    )(x, lhs, rhs, bcol, reward, head, gg)
     return reward, grad, head.T, gg[0]
 
 

time: 50.1 us -> 50.1 us (level)
  local copies, waits for them, and re-layouts: 6.83 us -> 0 us
  Pallas kernels: 41.8 us -> 48.6 us
    unnamed x4 -> x0, local copies, waits for them, and re-layouts: 6.83 us -> none
    pallas_call x0 -> x1, Pallas kernels: none -> 5.63 us  [on_device(): pl.pallas_call(finish, name='finish', out_shape=(jax.ShapeDtypeStruct((1,...]
    pallas_call x1, Pallas kernels: 41.8 us -> 43 us  [on_device(): pl.pallas_call(functools.partial(kernel, G, T, cap, scale, K, KR), name='...]
where the time goes in v2:
time: 50.1 us; the launch traced here: 49.9 us
  Pallas kernels  48.6 us (97%)
  between operations  1.29 us (3%)
    pallas_call x1, Pallas kernels, on_device(): pl.pallas_call(functools.partial(kernel, G, T, cap, scale, K, KR), name='...  43 us
    pallas_call x1, Pallas kernels, on_device(): pl.pallas_call(finish, name='finish', out_shape=(jax.ShapeDtypeStruct((1,...  5.63 us

profile of v2, /device:TPU:0, one launch (start us, length us, event | category | flops | bytes accessed | tf_op | source)
XLA Modules:
  0.0 49.9 jit_solution(2174489764833228209)
XLA Ops:
  1.3 43.0 %relay.1 = (f32[1,19]{1,0:T(1,128)}, bf16[384,2048]{1,0:T(8,128)(2,1)}, f32[19,2048]{1,0:T(8,128)}, f32[1,2048]{1,0:T(1,128)}, bf16[24,384]{1,0:T(8,128)(2,1)}, ...) custom-call(bf16[384,5120]{1,0:T(8,128)(2,1)} %hid_hbm.1, bf16[5120,2048]{1,0:T(8,128)(2,1)} %w_hbm.1, ...), custom_call_target="tpu_custom_call" | custom-call | tf_op jit(solution)/shard_map/relay/pallas_call | solution.py:347
  44.2 5.6 %finish.1 = (f32[1,19]{1,0:T(1,128)}, bf16[384,2048]{1,0:T(8,128)(2,1)}, f32[19,2048]{1,0:T(8,128)}, f32[1,2048]{1,0:T(1,128)}) custom-call(bf16[384,2048]{1,0:T(8,128)(2,1)} %get-tuple-element.15.x_hbm, bf16[24,384]{1,0:T(8,128)(2,1)} %get-tuple-element.16.lhs_ref, bf16[24,2048]{1,0:T(8,128)(2,1)} %get-tuple-element.17.rhs_ref, ...), custom_call_target="tpu_custom_call" | custom-call | tf_op jit(solution)/shard_map/finish/pallas_call | solution.py:388
